TPU v7x, 256 devices: a whole 4x4x8 slice. The times are simulated.
256 devices in a mesh: rows: 64 (over y, z, core), grp: 4 (over x).
Axes of the slice: x: 4, y: 4, z: 8, core: 2. Of those that a mesh axis runs over, the one named last changes fastest.
Arguments:
- panel: float32 [65536, 256], P(('rows', 'grp')), may hold values from -6000 to 6000
- trailing: float32 [65536, 2048], P(('rows', 'grp')), may hold values from -6000 to 6000
Outputs:
- upper_panel: float32 [256, 256], replicated
- projection: float32 [256, 2048], replicated
- updated: float32 [65536, 2048], P(('rows', 'grp'))
- upper_next: float32 [256, 256], replicated
All inputs are finite; a program needn't handle non-finite values.
Results may differ from a plain program's by a relative error of at most 0.00019.
Values sent between devices are 32-bit elements; how exact they have to be, the bound alone decides.
A program may use at most 128 MiB of HBM per device.

v0:
```python
import jax
import jax.numpy as jnp
from jax import lax
from jax.experimental import pallas as pl
from jax.experimental.pallas import tpu as pltpu
from jax.sharding import PartitionSpec as P

PB = 256
TC = 2048
WIDE = TC + 2 * PB
HALF = 128
SUB = 8
NX, NY, NZ = 4, 4, 8
INV_ROWS = 1.0 / 65536
VMEM = pl.BlockSpec(memory_space=pltpu.VMEM)


def dot(left, right, dims=(1, 0)):
    return lax.dot_general(
        left,
        right,
        (((dims[0],), (dims[1],)), ((), ())),
        precision=lax.Precision.HIGHEST,
        preferred_element_type=jnp.float32,
    )


def identity(order):
    rows = lax.broadcasted_iota(jnp.int32, (order, order), 0)
    columns = lax.broadcasted_iota(jnp.int32, (order, order), 1)
    return (rows == columns).astype(jnp.float32)


def aligned(value, step):
    return pl.multiple_of(value, step)


class Stream:
    def __init__(self, place, acc, out, first, width, x_first, split_z, bufs, send, recv):
        self.acc, self.out = acc, out
        self.columns = pl.ds(first, width)
        self.first, self.width, self.split_z = first, width, split_z
        self.core_buf, self.major_buf, self.minor_buf, self.z_buf = bufs
        self.send, self.recv = send, recv
        self.place = place
        x, y, z, core = place
        self.x_first = x_first
        self.major, self.minor = (x, y) if x_first else (y, x)
        self.base = core * 128
        self.slab = self.base + self.major * 32
        self.own = self.slab + self.minor * 8

    def device(self, axis, value):
        x, y, z, core = self.place
        if axis == "major":
            axis = "x" if self.x_first else "y"
        elif axis == "minor":
            axis = "y" if self.x_first else "x"
        if axis == "x":
            x = value
        elif axis == "y":
            y = value
        elif axis == "z":
            z = value
        else:
            core = value
        return ((y * NZ + z) * 2 + core, x)

    def rows(self, start, size):
        return pl.ds(aligned(start, 8), size)

    def piece(self, z):
        part = self.width // NZ
        return pl.ds(aligned(self.first + z * part, 128), part)

    def phase(self, name):
        acc, out, columns, z = self.acc, self.out, self.columns, self.place[2]
        other = 1 - self.place[3]
        if name == "core":
            return [(acc.at[self.rows(other * 128, 128), columns], self.core_buf, "core", other)]
        if name == "core_share":
            here = out.at[self.rows(self.base, 128), columns]
            return [(here, here, "core", other)]
        copies = []
        for d in range(1, NZ if name in ("z", "z_share") else 4):
            if name == "major":
                peer = lax.rem(self.major + d, 4)
                src = acc.at[self.rows(self.base + peer * 32, 32), columns]
                copies.append((src, self.major_buf.at[d - 1], "major", peer))
            elif name == "minor":
                peer = lax.rem(self.minor + d, 4)
                src = acc.at[self.rows(self.slab + peer * 8, 8), columns]
                copies.append((src, self.minor_buf.at[d - 1], "minor", peer))
            elif name == "z":
                peer = lax.rem(z + d, NZ)
                src = acc.at[self.rows(self.own, 8), self.piece(peer) if self.split_z else columns]
                copies.append((src, self.z_buf.at[d - 1], "z", peer))
            elif name == "z_share":
                here = out.at[self.rows(self.own, 8), self.piece(z)]
                copies.append((here, here, "z", lax.rem(z + d, NZ)))
            elif name == "minor_share":
                here = out.at[self.rows(self.own, 8), columns]
                copies.append((here, here, "minor", lax.rem(self.minor + d, 4)))
            else:
                here = out.at[self.rows(self.slab, 32), columns]
                copies.append((here, here, "major", lax.rem(self.major + d, 4)))
        return copies

    def copies(self, name):
        return [
            pltpu.make_async_remote_copy(
                src_ref=src,
                dst_ref=dst,
                send_sem=self.send.at[FIRST[name] + index],
                recv_sem=self.recv.at[FIRST[name] + index],
                device_id=self.device(axis, peer),
                device_id_type=pl.DeviceIdType.MESH,
            )
            for index, (src, dst, axis, peer) in enumerate(self.phase(name))
        ]

    def start(self, name):
        if name == "z_share" and not self.split_z:
            return
        for copy in self.copies(name):
            copy.start()

    def wait(self, name):
        if name == "z_share" and not self.split_z:
            return
        for copy in self.copies(name):
            copy.wait()

    def core_end(self):
        self.wait("core")

        @pl.loop(0, 16)
        def _(step):
            here = self.rows(self.base + step * 8, 8)
            there = pl.ds(aligned(step * 8, 8), 8)
            self.acc[here, self.columns] = self.acc[here, self.columns] + self.core_buf[there, :]

    def major_end(self):
        self.wait("major")

        @pl.loop(0, 4)
        def _(step):
            here = self.rows(self.slab + step * 8, 8)
            there = pl.ds(aligned(step * 8, 8), 8)
            total = self.acc[here, self.columns]
            for d in range(3):
                total = total + self.major_buf[d, there, :]
            self.acc[here, self.columns] = total

    def minor_end(self):
        self.wait("minor")
        here = self.rows(self.own, 8)
        total = self.acc[here, self.columns]
        for d in range(3):
            total = total + self.minor_buf[d]
        self.acc[here, self.columns] = total

    def z_end(self):
        self.wait("z")
        here = self.rows(self.own, 8)
        columns = self.piece(self.place[2]) if self.split_z else self.columns
        total = self.acc[here, columns]
        for d in range(NZ - 1):
            total = total + self.z_buf[d]
        self.out[here, columns] = total

    def turn(self, before, after):
        self.wait(before)
        self.start(after)


FIRST = {
    "core": 0,
    "major": 1,
    "minor": 4,
    "z": 7,
    "z_share": 14,
    "minor_share": 21,
    "major_share": 24,
    "core_share": 27,
}
COPIES = 28

CROSS = 2 * PB
STREAMS = ((0, 256, True, False), (256, 512, True, False), (768, 1024, True, True), (1792, 768, False, False))


def greet(place):
    x, y, z, core = place
    peers = [((y * NZ + z) * 2 + 1 - core, x)]
    peers += [((y * NZ + z) * 2 + core, lax.rem(x + d, NX)) for d in range(1, NX)]
    peers += [((lax.rem(y + d, NY) * NZ + z) * 2 + core, x) for d in range(1, NY)]
    peers += [((y * NZ + lax.rem(z + d, NZ)) * 2 + core, x) for d in range(1, NZ)]
    barrier = pltpu.get_barrier_semaphore()
    for peer in peers:
        pl.semaphore_signal(barrier, inc=1, device_id=peer, device_id_type=pl.DeviceIdType.MESH)
    return barrier, len(peers)


def factor_half(work, upper, inverse, between):
    full = (SUB, HALF)
    lane = lax.broadcasted_iota(jnp.int32, (1, HALF), 1)
    for block in range(HALF // SUB):
        between(block)
        base = block * SUB
        left = [jnp.broadcast_to(work[base + i : base + i + 1, :HALF], full) for i in range(SUB)]
        right = [jnp.broadcast_to(work[base + i : base + i + 1, HALF:], full) for i in range(SUB)]
        entry = [
            [jnp.broadcast_to(left[i][:, base + k : base + k + 1], full) for k in range(i + 1)]
            for i in range(SUB)
        ]
        unit = [[None] * SUB for _ in range(SUB)]
        recip = [None] * SUB
        for k in range(SUB):
            recip[k] = 1.0 / entry[k][k]
            for j in range(k + 1, SUB):
                unit[j][k] = entry[j][k] * recip[k]
            for j in range(k + 1, SUB):
                for i in range(j, SUB):
                    entry[i][j] = entry[i][j] - entry[i][k] * unit[j][k]
                left[j] = left[j] - unit[j][k] * left[k]
                right[j] = right[j] - unit[j][k] * right[k]
        for k in range(SUB):
            scale = lax.rsqrt(entry[k][k])
            row = base + k
            upper[row : row + 1, :] = jnp.where(lane >= row, (left[k] * scale)[0:1, :], 0.0)
            inverse[row : row + 1, :] = (right[k] * scale)[0:1, :]
        if base + SUB == HALF:
            break
        for k in range(SUB - 1, -1, -1):
            left[k] = left[k] * recip[k]
            right[k] = right[k] * recip[k]
            for j in range(k + 1, SUB):
                left[k] = left[k] - unit[j][k] * left[j]
                right[k] = right[k] - unit[j][k] * right[j]
        for other in range(base + SUB, HALF, SUB):
            rows = slice(other, other + SUB)
            lead = work[rows, :HALF]
            tail = work[rows, HALF:]
            column = [jnp.broadcast_to(lead[:, base + k : base + k + 1], full) for k in range(SUB)]
            for k in range(SUB):
                lead = lead - column[k] * left[k]
                tail = tail - column[k] * right[k]
            work[rows, :HALF] = lead
            work[rows, HALF:] = tail


def reduce_kernel(panel, trailing, out, upper, inverse, upper_next, acc, work, halves, inverses, middle, schur, *scratch):
    row = lax.axis_index("rows")
    x = lax.axis_index("grp")
    core = lax.rem(row, 2)
    z = lax.rem(row // 2, NZ)
    y = row // (2 * NZ)
    place = (x, y, z, core)
    barrier, greeted = greet(place)

    streams = []
    for index, (first, width, x_first, split_z) in enumerate(STREAMS):
        bufs, send, recv = scratch[6 * index : 6 * index + 4], *scratch[6 * index + 4 : 6 * index + 6]
        streams.append(Stream(place, acc, out, first, width, x_first, split_z, bufs, send, recv))
    gram, head, one, two = streams

    def products(first, last):
        @pl.loop(first, last)
        def _(tile):
            columns = pl.ds(aligned(tile * PB, PB), PB)
            acc[:, pl.ds(aligned(CROSS + tile * PB, PB), PB)] = dot(panel[...], trailing[:, columns], (0, 0))

    acc[:, :PB] = dot(panel[...], panel[...], (0, 0))
    pl.semaphore_wait(barrier, greeted)
    gram.start("core")
    acc[:, PB : 2 * PB] = dot(trailing[:, :PB], trailing[:, :PB], (0, 0))
    gram.core_end()
    gram.start("major")
    acc[:, CROSS : CROSS + PB] = dot(panel[...], trailing[:, :PB], (0, 0))
    head.start("core")
    products(1, 5)
    head.core_end()
    one.start("core")
    gram.major_end()
    gram.start("minor")
    head.start("major")
    products(5, TC // PB)
    two.start("core")
    gram.minor_end()
    gram.start("z")
    one.core_end()
    head.major_end()
    head.start("minor")
    one.start("major")
    two.core_end()
    gram.z_end()
    gram.start("minor_share")
    head.minor_end()
    head.start("z")
    gram.turn("minor_share", "major_share")
    two.start("major")
    gram.turn("major_share", "core_share")
    head.z_end()
    head.start("minor_share")
    gram.wait("core_share")

    def meet_first():
        head.turn("minor_share", "major_share")
        one.major_end()
        one.start("minor")

    def meet_second():
        head.turn("major_share", "core_share")
        two.major_end()
        two.start("minor")

    def meet_third():
        one.minor_end()
        one.start("z")

    def meet_fourth():
        two.minor_end()
        two.start("z")

    def meet_fifth():
        one.z_end()
        one.start("z_share")
        two.z_end()
        two.start("minor_share")

    def meet_sixth():
        head.wait("core_share")
        one.turn("z_share", "minor_share")
        two.turn("minor_share", "major_share")

    def meet_seventh():
        one.turn("minor_share", "major_share")

    def meet_eighth():
        two.turn("major_share", "core_share")

    def meet_last():
        one.turn("major_share", "core_share")

    meetings = (
        (0, 2, meet_first),
        (0, 10, meet_second),
        (0, 14, meet_third),
        (1, 2, meet_fourth),
        (1, 9, meet_fifth),
        (1, 15, meet_sixth),
        (2, 10, meet_seventh),
        (3, 2, meet_eighth),
        (3, 12, meet_last),
    )

    zeros = jnp.zeros((HALF, HALF), jnp.float32)
    work[:, :HALF] = out[:HALF, :HALF] * INV_ROWS
    work[:, HALF:] = identity(HALF)
    schur[...] = out[:, :PB] * INV_ROWS

    @pl.loop(0, 4)
    def _(step):
        @pl.when(lax.rem(step, 2) == 1)
        def _():
            cross = dot(inverses[0], schur[:HALF, HALF:])
            middle[...] = cross
            work[:, :HALF] = schur[HALF:, HALF:] - dot(cross, cross, (0, 0))
            work[:, HALF:] = identity(HALF)

        @pl.when(step == 2)
        def _():
            upper[:HALF, :HALF] = halves[0]
            upper[:HALF, HALF:] = middle[...]
            upper[HALF:, :HALF] = zeros
            upper[HALF:, HALF:] = halves[1]
            inverse[:HALF, :HALF] = inverses[0]
            inverse[:HALF, HALF:] = zeros
            inverse[HALF:, :HALF] = -dot(inverses[1], dot(middle[...], inverses[0], (0, 0)))
            inverse[HALF:, HALF:] = inverses[1]
            part = dot(inverse[...], out[:, CROSS : CROSS + PB] * INV_ROWS)
            schur[...] = out[:, PB : 2 * PB] * INV_ROWS - dot(part, part, (0, 0))
            work[:, :HALF] = schur[:HALF, :HALF]
            work[:, HALF:] = identity(HALF)

        def between(block):
            for at_step, at_block, action in meetings:
                if at_block == block:
                    pl.when(step == at_step)(action)

        at = lax.rem(step, 2)
        factor_half(work, halves.at[at], inverses.at[at], between)

    upper_next[:HALF, :HALF] = halves[0]
    upper_next[:HALF, HALF:] = middle[...]
    upper_next[HALF:, :HALF] = zeros
    upper_next[HALF:, HALF:] = halves[1]
    one.wait("core_share")
    two.wait("core_share")


def reduced(panel, trailing):
    square = jax.ShapeDtypeStruct((PB, PB), jnp.float32)
    scratch = [
        pltpu.VMEM((PB, WIDE), jnp.float32),
        pltpu.VMEM((HALF, PB), jnp.float32),
        pltpu.VMEM((2, HALF, HALF), jnp.float32),
        pltpu.VMEM((2, HALF, HALF), jnp.float32),
        pltpu.VMEM((HALF, HALF), jnp.float32),
        pltpu.VMEM((PB, PB), jnp.float32),
    ]
    for _, width, _, split_z in STREAMS:
        part = width // NZ if split_z else width
        scratch += [
            pltpu.VMEM((128, width), jnp.float32),
            pltpu.VMEM((3, 32, width), jnp.float32),
            pltpu.VMEM((3, 8, width), jnp.float32),
            pltpu.VMEM((NZ - 1, 8, part), jnp.float32),
            pltpu.SemaphoreType.DMA((COPIES,)),
            pltpu.SemaphoreType.DMA((COPIES,)),
        ]
    return pl.pallas_call(
        reduce_kernel,
        out_shape=(jax.ShapeDtypeStruct((PB, WIDE), jnp.float32), square, square, square),
        in_specs=[VMEM, VMEM],
        out_specs=(VMEM, VMEM, VMEM, VMEM),
        scratch_shapes=scratch,
        compiler_params=pltpu.CompilerParams(
            collective_id=0, has_side_effects=True, vmem_limit_bytes=40 * 2**20
        ),
        cost_estimate=pl.CostEstimate(flops=600_000_000, bytes_accessed=6_000_000, transcendentals=600),
        name="reduce",
    )(panel, trailing)


def update_kernel(panel, inverse, sums, trailing, factor, factor_next, projection, updated, upper, upper_next, basis):
    at = pl.program_id(0) * TILE

    @pl.when(pl.program_id(0) == 0)
    def _():
        basis[...] = dot(panel[...], inverse[...], (1, 1))
        upper[...] = factor[...]
        upper_next[...] = factor_next[...]

    coefficients = dot(inverse[...], sums[:, pl.ds(aligned(CROSS + at, PB), TILE)] * INV_ROWS)
    projection[...] = coefficients
    updated[...] = trailing[:, pl.ds(aligned(at, PB), TILE)] - dot(basis[...], coefficients)


TILE = 512


def update(panel, inverse, sums, trailing, factor, factor_next):
    wide = jax.ShapeDtypeStruct((PB, TC), jnp.float32)
    square = jax.ShapeDtypeStruct((PB, PB), jnp.float32)
    whole = pl.BlockSpec((PB, PB), lambda i: (0, 0))
    tile = pl.BlockSpec((PB, TILE), lambda i: (0, i))
    return pl.pallas_call(
        update_kernel,
        out_shape=(wide, wide, square, square),
        grid=(TC // TILE,),
        in_specs=[VMEM] * 6,
        out_specs=(tile, tile, whole, whole),
        scratch_shapes=[pltpu.VMEM((PB, PB), jnp.float32)],
        compiler_params=pltpu.CompilerParams(vmem_limit_bytes=24 * 2**20),
        cost_estimate=pl.CostEstimate(flops=600_000_000, bytes_accessed=9_000_000, transcendentals=0),
        name="update",
    )(panel, inverse, sums, trailing, factor, factor_next)


def per_device(panel, trailing):
    sums, factor, inverse, factor_next = reduced(panel, trailing)
    projection, updated, upper_panel, upper_next = update(panel, inverse, sums, trailing, factor, factor_next)
    return (upper_panel, projection, updated, upper_next)


def solution(mesh):
    return jax.shard_map(
        per_device,
        mesh=mesh,
        in_specs=(P(("rows", "grp"), None), P(("rows", "grp"), None)),
        out_specs=(P(), P(), P(("rows", "grp"), None), P()),
        check_vma=False,
    )
```

profile of v0, /device:TPU:1, one launch (start us, length us, event | category | flops | bytes accessed | tf_op | source)
XLA Modules:
  0.0 78.5 jit_solution(10134418296450955314)
XLA Ops:
  0.6 0.0 copy-start
  0.6 1.6 %copy-done = f32[256,2048]{1,0:T(8,128)S(1)} copy-done((f32[256,2048]{1,0:T(8,128)S(1)}, f32[256,2048]{1,0:T(8,128)}, u32[]{:S(2)}) %copy-start) | copy-done | bytes 2097176
  2.2 0.0 copy-start.1
  2.2 0.9 %copy-done.1 = f32[256,256]{1,0:T(8,128)S(1)} copy-done((f32[256,256]{1,0:T(8,128)S(1)}, f32[256,256]{1,0:T(8,128)}, u32[]{:S(2)}) %copy-start.1) | copy-done | bytes 262168
  3.2 69.1 %reduce.1 = (f32[256,2560]{1,0:T(8,128)S(1)}, f32[256,256]{1,0:T(8,128)S(1)}, f32[256,256]{1,0:T(8,128)S(1)}, f32[256,256]{1,0:T(8,128)S(1)}) custom-call(f32[256,256]{1,0:T(8,128)S(1)} %copy-done.1, f32[256,2048]{1,0:T(8,128)S(1)} %copy-done), custom_call_target="tpu_custom_call" | custom-call | flops 600000000 | bytes 6000000 | tf_op jit(solution)/shard_map/reduce/pallas_call | solution.py:423
  72.3 6.2 %update.1 = (f32[256,2048]{1,0:T(8,128)}, f32[256,2048]{1,0:T(8,128)}, f32[256,256]{1,0:T(8,128)}, f32[256,256]{1,0:T(8,128)}) custom-call(f32[256,256]{1,0:T(8,128)S(1)} %copy-done.1, f32[256,256]{1,0:T(8,128)S(1)} %get-tuple-element.12.inverse, f32[256,2560]{1,0:T(8,128)S(1)} %get-tuple-element.13.sums, f32[256,2048]{1,0:T(8,128)S(1)} %copy-done, ...), custom_call_target="tpu_custom_call" | custom-call | flops 600000000 | bytes 9000000 | tf_op jit(solution)/shard_map/update/pallas_call | solution.py:459
Async XLA Ops:
  0.6 1.6 %copy-start = (f32[256,2048]{1,0:T(8,128)S(1)}, f32[256,2048]{1,0:T(8,128)}, u32[]{:S(2)}) copy-start(f32[256,2048]{1,0:T(8,128)} %trailing.3) | copy-start | bytes 6291460
  2.2 0.9 %copy-start.1 = (f32[256,256]{1,0:T(8,128)S(1)}, f32[256,256]{1,0:T(8,128)}, u32[]{:S(2)}) copy-start(f32[256,256]{1,0:T(8,128)} %panel.3) | copy-start | bytes 786436
where the time goes:
time: 78.6 us; the launch traced here: 78.5 us
  Pallas kernels  75.3 us (96%)
  local copies, waits for them, and re-layouts  2.53 us (3%)
    pallas_call x1, Pallas kernels, reduced(): pl.pallas_call(reduce_kernel, out_shape=(jax.ShapeDtypeStruct((PB, WIDE),...  69.1 us
    pallas_call x1, Pallas kernels, update(): pl.pallas_call(update_kernel, out_shape=(wide, wide, square, square), gri...  6.17 us
    unnamed x4, local copies, waits for them, and re-layouts  2.53 us

commit v1 on v0

--- a/solution.py
+++ b/solution.py
@@ -187,7 +187,7 @@
 COPIES = 28
 
 CROSS = 2 * PB
-STREAMS = ((0, 256, True, False), (256, 512, True, False), (768, 1024, True, True), (1792, 768, False, False))
+STREAMS = ((0, 256, True, False), (256, 512, False, False), (768, 1024, True, True), (1792, 768, False, False))
 
 
 def greet(place):
@@ -275,84 +275,81 @@
     pl.semaphore_wait(barrier, greeted)
     gram.start("core")
     acc[:, PB : 2 * PB] = dot(trailing[:, :PB], trailing[:, :PB], (0, 0))
+    acc[:, CROSS : CROSS + PB] = dot(panel[...], trailing[:, :PB], (0, 0))
     gram.core_end()
     gram.start("major")
-    acc[:, CROSS : CROSS + PB] = dot(panel[...], trailing[:, :PB], (0, 0))
     head.start("core")
     products(1, 5)
+    one.start("core")
     head.core_end()
-    one.start("core")
+    head.start("major")
     gram.major_end()
     gram.start("minor")
-    head.start("major")
+    one.core_end()
+    one.start("major")
     products(5, TC // PB)
     two.start("core")
     gram.minor_end()
     gram.start("z")
-    one.core_end()
+    two.core_end()
+    two.start("major")
     head.major_end()
     head.start("minor")
-    one.start("major")
-    two.core_end()
     gram.z_end()
     gram.start("minor_share")
     head.minor_end()
     head.start("z")
+    one.major_end()
+    one.start("minor")
+    two.major_end()
+    two.start("minor")
     gram.turn("minor_share", "major_share")
-    two.start("major")
+    one.minor_end()
+    one.start("z")
+    two.minor_end()
+    two.start("z")
     gram.turn("major_share", "core_share")
     head.z_end()
     head.start("minor_share")
     gram.wait("core_share")
 
     def meet_first():
-        head.turn("minor_share", "major_share")
-        one.major_end()
-        one.start("minor")
-
-    def meet_second():
-        head.turn("major_share", "core_share")
-        two.major_end()
-        two.start("minor")
-
-    def meet_third():
-        one.minor_end()
-        one.start("z")
-
-    def meet_fourth():
-        two.minor_end()
-        two.start("z")
-
-    def meet_fifth():
         one.z_end()
         one.start("z_share")
+
+    def meet_second():
+        head.turn("minor_share", "major_share")
+
+    def meet_third():
         two.z_end()
         two.start("minor_share")
+        one.turn("z_share", "minor_share")
+
+    def meet_fourth():
+        head.turn("major_share", "core_share")
+
+    def meet_fifth():
+        two.turn("minor_share", "major_share")
 
     def meet_sixth():
+        one.turn("minor_share", "major_share")
         head.wait("core_share")
-        one.turn("z_share", "minor_share")
-        two.turn("minor_share", "major_share")
 
     def meet_seventh():
-        one.turn("minor_share", "major_share")
-
-    def meet_eighth():
         two.turn("major_share", "core_share")
 
     def meet_last():
         one.turn("major_share", "core_share")
 
     meetings = (
-        (0, 2, meet_first),
-        (0, 10, meet_second),
-        (0, 14, meet_third),
-        (1, 2, meet_fourth),
-        (1, 9, meet_fifth),
+        (0, 3, meet_first),
+        (0, 6, meet_second),
+        (1, 2, meet_third),
+        (1, 7, meet_fourth),
+        (1, 12, meet_fifth),
         (1, 15, meet_sixth),
-        (2, 10, meet_seventh),
-        (3, 2, meet_eighth),
-        (3, 12, meet_last),
+        (3, 2, meet_seventh),
+        (3, 9, meet_last),
     )
 
     zeros = jnp.zeros((HALF, HALF), jnp.float32)

time: 78.6 us -> 65.5 us (0.83)
  Pallas kernels: 75.3 us -> 62.2 us
    pallas_call x1, Pallas kernels: 69.1 us -> 56 us  [reduced(): pl.pallas_call(reduce_kernel, out_shape=(jax.ShapeDtypeStruct((PB, WIDE),...]
where the time goes in v1:
time: 65.5 us; the launch traced here: 65.4 us
  Pallas kernels  62.2 us (95%)
  local copies, waits for them, and re-layouts  2.53 us (4%)
    pallas_call x1, Pallas kernels, reduced(): pl.pallas_call(reduce_kernel, out_shape=(jax.ShapeDtypeStruct((PB, WIDE),...  56 us
    pallas_call x1, Pallas kernels, update(): pl.pallas_call(update_kernel, out_shape=(wide, wide, square, square), gri...  6.17 us
    unnamed x4, local copies, waits for them, and re-layouts  2.53 us

profile of v1, /device:TPU:1, one launch (start us, length us, event | category | flops | bytes accessed | tf_op | source)
XLA Modules:
  0.0 65.4 jit_solution(6528754999512820059)
XLA Ops:
  0.6 0.0 copy-start
  0.6 1.6 %copy-done = f32[256,2048]{1,0:T(8,128)S(1)} copy-done((f32[256,2048]{1,0:T(8,128)S(1)}, f32[256,2048]{1,0:T(8,128)}, u32[]{:S(2)}) %copy-start) | copy-done | bytes 2097176
  2.2 0.0 copy-start.1
  2.2 0.9 %copy-done.1 = f32[256,256]{1,0:T(8,128)S(1)} copy-done((f32[256,256]{1,0:T(8,128)S(1)}, f32[256,256]{1,0:T(8,128)}, u32[]{:S(2)}) %copy-start.1) | copy-done | bytes 262168
  3.2 56.0 %reduce.1 = (f32[256,2560]{1,0:T(8,128)S(1)}, f32[256,256]{1,0:T(8,128)S(1)}, f32[256,256]{1,0:T(8,128)S(1)}, f32[256,256]{1,0:T(8,128)S(1)}) custom-call(f32[256,256]{1,0:T(8,128)S(1)} %copy-done.1, f32[256,2048]{1,0:T(8,128)S(1)} %copy-done), custom_call_target="tpu_custom_call" | custom-call | flops 600000000 | bytes 6000000 | tf_op jit(solution)/shard_map/reduce/pallas_call | solution.py:420
  59.2 6.2 %update.1 = (f32[256,2048]{1,0:T(8,128)}, f32[256,2048]{1,0:T(8,128)}, f32[256,256]{1,0:T(8,128)}, f32[256,256]{1,0:T(8,128)}) custom-call(f32[256,256]{1,0:T(8,128)S(1)} %copy-done.1, f32[256,256]{1,0:T(8,128)S(1)} %get-tuple-element.12.inverse, f32[256,2560]{1,0:T(8,128)S(1)} %get-tuple-element.13.sums, f32[256,2048]{1,0:T(8,128)S(1)} %copy-done, ...), custom_call_target="tpu_custom_call" | custom-call | flops 600000000 | bytes 9000000 | tf_op jit(solution)/shard_map/update/pallas_call | solution.py:456
Async XLA Ops:
  0.6 1.6 %copy-start = (f32[256,2048]{1,0:T(8,128)S(1)}, f32[256,2048]{1,0:T(8,128)}, u32[]{:S(2)}) copy-start(f32[256,2048]{1,0:T(8,128)} %trailing.3) | copy-start | bytes 6291460
  2.2 0.9 %copy-start.1 = (f32[256,256]{1,0:T(8,128)S(1)}, f32[256,256]{1,0:T(8,128)}, u32[]{:S(2)}) copy-start(f32[256,256]{1,0:T(8,128)} %panel.3) | copy-start | bytes 786436

commit v2 on v1

--- a/solution.py
+++ b/solution.py
@@ -202,7 +202,7 @@
     return barrier, len(peers)
 
 
-def factor_half(work, upper, inverse, between):
+def factor_half(work, upper, inverse, between, inverted):
     full = (SUB, HALF)
     lane = lax.broadcasted_iota(jnp.int32, (1, HALF), 1)
     for block in range(HALF // SUB):
@@ -224,20 +224,24 @@
                 for i in range(j, SUB):
                     entry[i][j] = entry[i][j] - entry[i][k] * unit[j][k]
                 left[j] = left[j] - unit[j][k] * left[k]
-                right[j] = right[j] - unit[j][k] * right[k]
+                if inverted:
+                    right[j] = right[j] - unit[j][k] * right[k]
         for k in range(SUB):
             scale = lax.rsqrt(entry[k][k])
             row = base + k
             upper[row : row + 1, :] = jnp.where(lane >= row, (left[k] * scale)[0:1, :], 0.0)
-            inverse[row : row + 1, :] = (right[k] * scale)[0:1, :]
+            if inverted:
+                inverse[row : row + 1, :] = (right[k] * scale)[0:1, :]
         if base + SUB == HALF:
             break
         for k in range(SUB - 1, -1, -1):
             left[k] = left[k] * recip[k]
-            right[k] = right[k] * recip[k]
             for j in range(k + 1, SUB):
                 left[k] = left[k] - unit[j][k] * left[j]
-                right[k] = right[k] - unit[j][k] * right[j]
+            if inverted:
+                right[k] = right[k] * recip[k]
+                for j in range(k + 1, SUB):
+                    right[k] = right[k] - unit[j][k] * right[j]
         for other in range(base + SUB, HALF, SUB):
             rows = slice(other, other + SUB)
             lead = work[rows, :HALF]
@@ -245,18 +249,44 @@
             column = [jnp.broadcast_to(lead[:, base + k : base + k + 1], full) for k in range(SUB)]
             for k in range(SUB):
                 lead = lead - column[k] * left[k]
-                tail = tail - column[k] * right[k]
+                if inverted:
+                    tail = tail - column[k] * right[k]
             work[rows, :HALF] = lead
-            work[rows, HALF:] = tail
-
-
-def reduce_kernel(panel, trailing, out, upper, inverse, upper_next, acc, work, halves, inverses, middle, schur, *scratch):
+            if inverted:
+                work[rows, HALF:] = tail
+
+
+def reduce_kernel(
+    panel_hbm,
+    trailing_hbm,
+    out,
+    upper,
+    inverse,
+    upper_next,
+    basis,
+    panel,
+    trailing,
+    load,
+    acc,
+    work,
+    halves,
+    inverses,
+    middle,
+    schur,
+    *scratch,
+):
     row = lax.axis_index("rows")
     x = lax.axis_index("grp")
     core = lax.rem(row, 2)
     z = lax.rem(row // 2, NZ)
     y = row // (2 * NZ)
     place = (x, y, z, core)
+    loads = [
+        pltpu.make_async_copy(panel_hbm, panel, load.at[0]),
+        pltpu.make_async_copy(trailing_hbm, trailing, load.at[1]),
+    ]
+    for copy in loads:
+        copy.start()
     barrier, greeted = greet(place)
 
     streams = []
@@ -271,7 +301,9 @@
             columns = pl.ds(aligned(tile * PB, PB), PB)
             acc[:, pl.ds(aligned(CROSS + tile * PB, PB), PB)] = dot(panel[...], trailing[:, columns], (0, 0))
 
+    loads[0].wait()
     acc[:, :PB] = dot(panel[...], panel[...], (0, 0))
+    loads[1].wait()
     pl.semaphore_wait(barrier, greeted)
     gram.start("core")
     acc[:, PB : 2 * PB] = dot(trailing[:, :PB], trailing[:, :PB], (0, 0))
@@ -357,17 +389,13 @@
     work[:, HALF:] = identity(HALF)
     schur[...] = out[:, :PB] * INV_ROWS
 
-    @pl.loop(0, 4)
-    def _(step):
-        @pl.when(lax.rem(step, 2) == 1)
-        def _():
+    for step in range(4):
+        if step % 2 == 1:
             cross = dot(inverses[0], schur[:HALF, HALF:])
             middle[...] = cross
             work[:, :HALF] = schur[HALF:, HALF:] - dot(cross, cross, (0, 0))
             work[:, HALF:] = identity(HALF)
-
-        @pl.when(step == 2)
-        def _():
+        if step == 2:
             upper[:HALF, :HALF] = halves[0]
             upper[:HALF, HALF:] = middle[...]
             upper[HALF:, :HALF] = zeros
@@ -383,23 +411,26 @@
 
         def between(block):
             for at_step, at_block, action in meetings:
-                if at_block == block:
-                    pl.when(step == at_step)(action)
-
-        at = lax.rem(step, 2)
-        factor_half(work, halves.at[at], inverses.at[at], between)
+                if at_step == step and at_block == block:
+                    action()
+
+        factor_half(work, halves.at[step % 2], inverses.at[step % 2], between, step < 3)
 
     upper_next[:HALF, :HALF] = halves[0]
     upper_next[:HALF, HALF:] = middle[...]
     upper_next[HALF:, :HALF] = zeros
     upper_next[HALF:, HALF:] = halves[1]
+    basis[...] = dot(panel[...], inverse[...], (1, 1))
+    two.wait("core_share")
     one.wait("core_share")
-    two.wait("core_share")
 
 
 def reduced(panel, trailing):
     square = jax.ShapeDtypeStruct((PB, PB), jnp.float32)
     scratch = [
+        pltpu.VMEM((PB, PB), jnp.float32),
+        pltpu.VMEM((PB, TC), jnp.float32),
+        pltpu.SemaphoreType.DMA((2,)),
         pltpu.VMEM((PB, WIDE), jnp.float32),
         pltpu.VMEM((HALF, PB), jnp.float32),
         pltpu.VMEM((2, HALF, HALF), jnp.float32),
@@ -419,9 +450,9 @@
         ]
     return pl.pallas_call(
         reduce_kernel,
-        out_shape=(jax.ShapeDtypeStruct((PB, WIDE), jnp.float32), square, square, square),
-        in_specs=[VMEM, VMEM],
-        out_specs=(VMEM, VMEM, VMEM, VMEM),
+        out_shape=(jax.ShapeDtypeStruct((PB, WIDE), jnp.float32), square, square, square, square),
+        in_specs=[pl.BlockSpec(memory_space=pltpu.HBM)] * 2,
+        out_specs=(VMEM, VMEM, VMEM, VMEM, VMEM),
         scratch_shapes=scratch,
         compiler_params=pltpu.CompilerParams(
             collective_id=0, has_side_effects=True, vmem_limit_bytes=40 * 2**20
@@ -431,24 +462,35 @@
     )(panel, trailing)
 
 
-def update_kernel(panel, inverse, sums, trailing, factor, factor_next, projection, updated, upper, upper_next, basis):
+def halves_of(value):
+    high = value.astype(jnp.bfloat16)
+    return high, (value - high.astype(jnp.float32)).astype(jnp.bfloat16)
+
+
+def product(left, right):
+    return jnp.dot(left, right, preferred_element_type=jnp.float32)
+
+
+def update_kernel(basis, inverse, sums, trailing, factor, factor_next, projection, updated, upper, upper_next, coarse, fine):
     at = pl.program_id(0) * TILE
 
     @pl.when(pl.program_id(0) == 0)
     def _():
-        basis[...] = dot(panel[...], inverse[...], (1, 1))
         upper[...] = factor[...]
         upper_next[...] = factor_next[...]
+        coarse[...], fine[...] = halves_of(basis[...])
 
     coefficients = dot(inverse[...], sums[:, pl.ds(aligned(CROSS + at, PB), TILE)] * INV_ROWS)
     projection[...] = coefficients
-    updated[...] = trailing[:, pl.ds(aligned(at, PB), TILE)] - dot(basis[...], coefficients)
+    high, low = halves_of(coefficients)
+    span = product(coarse[...], high) + (product(coarse[...], low) + product(fine[...], high))
+    updated[...] = trailing[:, pl.ds(aligned(at, PB), TILE)] - span
 
 
 TILE = 512
 
 
-def update(panel, inverse, sums, trailing, factor, factor_next):
+def update(basis, inverse, sums, trailing, factor, factor_next):
     wide = jax.ShapeDtypeStruct((PB, TC), jnp.float32)
     square = jax.ShapeDtypeStruct((PB, PB), jnp.float32)
     whole = pl.BlockSpec((PB, PB), lambda i: (0, 0))
@@ -459,16 +501,16 @@
         grid=(TC // TILE,),
         in_specs=[VMEM] * 6,
         out_specs=(tile, tile, whole, whole),
-        scratch_shapes=[pltpu.VMEM((PB, PB), jnp.float32)],
+        scratch_shapes=[pltpu.VMEM((PB, PB), jnp.bfloat16)] * 2,
         compiler_params=pltpu.CompilerParams(vmem_limit_bytes=24 * 2**20),
         cost_estimate=pl.CostEstimate(flops=600_000_000, bytes_accessed=9_000_000, transcendentals=0),
         name="update",
-    )(panel, inverse, sums, trailing, factor, factor_next)
+    )(basis, inverse, sums, trailing, factor, factor_next)
 
 
 def per_device(panel, trailing):
-    sums, factor, inverse, factor_next = reduced(panel, trailing)
-    projection, updated, upper_panel, upper_next = update(panel, inverse, sums, trailing, factor, factor_next)
+    sums, factor, inverse, factor_next, basis = reduced(panel, trailing)
+    projection, updated, upper_panel, upper_next = update(basis, inverse, sums, trailing, factor, factor_next)
     return (upper_panel, projection, updated, upper_next)
 
 

time: 65.5 us -> 63.9 us (0.976)
  Pallas kernels: 62.2 us -> 60.6 us
    pallas_call x1, Pallas kernels: 6.17 us -> 4.87 us  [update(): pl.pallas_call(update_kernel, out_shape=(wide, wide, square, square), gri...]
where the time goes in v2:
time: 63.9 us; the launch traced here: 63.8 us
  Pallas kernels  60.6 us (95%)
  local copies, waits for them, and re-layouts  2.53 us (4%)
  between operations  0.65 us (1%)
    pallas_call x1, Pallas kernels, reduced(): pl.pallas_call(reduce_kernel, out_shape=(jax.ShapeDtypeStruct((PB, WIDE),...  55.7 us
    pallas_call x1, Pallas kernels, update(): pl.pallas_call(update_kernel, out_shape=(wide, wide, square, square), gri...  4.87 us
    unnamed x4, local copies, waits for them, and re-layouts  2.53 us

profile of v2, /device:TPU:1, one launch (start us, length us, event | category | flops | bytes accessed | tf_op | source)
XLA Modules:
  0.0 63.8 jit_solution(15199141138784842257)
XLA Ops:
  0.6 0.0 copy-start
  0.6 1.6 %copy-done = f32[256,2048]{1,0:T(8,128)S(1)} copy-done((f32[256,2048]{1,0:T(8,128)S(1)}, f32[256,2048]{1,0:T(8,128)}, u32[]{:S(2)}) %copy-start) | copy-done | bytes 2097176
  2.2 0.0 copy-start.1
  2.2 0.9 %copy-done.1 = f32[256,256]{1,0:T(8,128)S(1)} copy-done((f32[256,256]{1,0:T(8,128)S(1)}, f32[256,256]{1,0:T(8,128)}, u32[]{:S(2)}) %copy-start.1) | copy-done | bytes 262168
  3.2 55.7 %reduce.1 = (f32[256,2560]{1,0:T(8,128)S(1)}, f32[256,256]{1,0:T(8,128)S(1)}, f32[256,256]{1,0:T(8,128)S(1)}, f32[256,256]{1,0:T(8,128)S(1)}, f32[256,256]{1,0:T(8,128)S(1)}) custom-call(f32[256,256]{1,0:T(8,128)S(1)} %copy-done.1, f32[256,2048]{1,0:T(8,128)S(1)} %copy-done), custom_call_target="tpu_custom_call" | custom-call | flops 600000000 | bytes 6000000 | tf_op jit(solution)/shard_map/reduce/pallas_call | solution.py:451
  58.9 4.9 %update.1 = (f32[256,2048]{1,0:T(8,128)}, f32[256,2048]{1,0:T(8,128)}, f32[256,256]{1,0:T(8,128)}, f32[256,256]{1,0:T(8,128)}) custom-call(f32[256,256]{1,0:T(8,128)S(1)} %get-tuple-element.13.basis, f32[256,256]{1,0:T(8,128)S(1)} %get-tuple-element.14.inverse, f32[256,2560]{1,0:T(8,128)S(1)} %get-tuple-element.15.sums, f32[256,2048]{1,0:T(8,128)S(1)} %copy-done, ...), custom_call_target="tpu_custom_call" | custom-call | flops 600000000 | bytes 9000000 | tf_op jit(solution)/shard_map/update/pallas_call | solution.py:498
Async XLA Ops:
  0.6 1.6 %copy-start = (f32[256,2048]{1,0:T(8,128)S(1)}, f32[256,2048]{1,0:T(8,128)}, u32[]{:S(2)}) copy-start(f32[256,2048]{1,0:T(8,128)} %trailing.1) | copy-start | bytes 6291460
  2.2 0.9 %copy-start.1 = (f32[256,256]{1,0:T(8,128)S(1)}, f32[256,256]{1,0:T(8,128)}, u32[]{:S(2)}) copy-start(f32[256,256]{1,0:T(8,128)} %panel_hbm.1) | copy-start | bytes 786436
